TPU v7x, 32 devices: a whole 2x2x4 slice. The times are simulated.
32 devices in a mesh: tm: 4 (over y, core), rows: 8 (over z, x).
Axes of the slice: x: 2, y: 2, z: 4, core: 2. Of those that a mesh axis runs over, the one named last changes fastest.
Arguments:
- features: bfloat16 [4, 24, 64, 512], P('tm', 'rows'), may hold values from -64 to 64, as said below
- gamma: float32 [512], replicated, may hold values from 0.1 to 1.9
- beta: float32 [512], replicated, may hold values from -3 to 3
- kernel: bfloat16 [3, 512, 3, 3, 512], P(None, 'tm'), may hold values from -0.0546875 to 0.0546875
- bias: float32 [512], replicated, may hold values from -3 to 3
Outputs:
- decoded: bfloat16 [4, 24, 64, 512], P('tm', 'rows')
Inputs may be any that keep to these rules, and one draw needn't show every extreme that they name: features are finite.
All inputs are finite; a program needn't handle non-finite values.
Results may differ from a plain program's by a relative error of at most 0.004.
Values may be sent and summed in bfloat16 or wider, within the bound.
A program may use at most 128 MiB of HBM per device.

v0:
```python
import jax
import jax.numpy as jnp
from jax import lax
from jax.sharding import PartitionSpec as P

GROUPS = 32
EPSILON = 1e-06


def shifted(x, axis, by):
    length = lax.axis_size(axis)
    pairs = [(i, i + by) for i in range(length) if 0 <= i + by < length]
    return lax.ppermute(x, axis, pairs)


def extended_2(x, sides, width):
    for axis, dim in sides:
        size, length = (lax.axis_size(axis), x.shape[dim])
        up = [(i, (i + 1) % size) for i in range(size - 1)]
        down = [(j, i) for i, j in up]
        last = lax.slice_in_dim(x, length - width, length, axis=dim)
        first = lax.slice_in_dim(x, 0, width, axis=dim)
        before = lax.ppermute(last, axis, up)
        after = lax.ppermute(first, axis, down)
        x = jnp.concatenate([before, x, after], axis=dim)
    return x


def unfold(block, height, across):
    pieces = []
    for tap_row in range(3):
        for tap_col in range(3):
            pieces.append(block[:, tap_row : tap_row + height, tap_col : tap_col + across, :])
    return jnp.concatenate(pieces, axis=-1)


def flatten_taps(taps):
    return taps.reshape(3, taps.shape[1], -1)


def apply_taps(columns, taps, frames):
    flat = flatten_taps(taps)
    total = jnp.einsum(
        "fhwc,kc->fhwk", columns[0:frames], flat[0], preferred_element_type=jnp.float32
    )
    for tap_time in (1, 2):
        total = total + jnp.einsum(
            "fhwc,kc->fhwk",
            columns[tap_time : tap_time + frames],
            flat[tap_time],
            preferred_element_type=jnp.float32,
        )
    return total


def widen(block):
    return jnp.pad(block, ((0, 0), (0, 0), (1, 1), (0, 0)))


def previous_span(block):
    return shifted(block, "tm", 1)


def local(features, gamma, beta, kernel, bias):
    frames, height, across, channels = features.shape
    values = features.astype(jnp.float32)
    grouped = values.reshape(frames, height, across, GROUPS, channels // GROUPS)
    count = float(
        frames
        * height
        * across
        * (channels // GROUPS)
        * lax.axis_size("tm")
        * lax.axis_size("rows")
    )
    totals, squares = lax.psum(
        (jnp.sum(grouped, axis=(0, 1, 2, 4)), jnp.sum(grouped * grouped, axis=(0, 1, 2, 4))),
        ("tm", "rows"),
    )
    center = totals / count
    spread = squares / count - center * center
    centered = grouped - center[:, None]
    normed = (centered * lax.rsqrt(spread + EPSILON)[:, None]).reshape(
        frames, height, across, channels
    )
    active = jax.nn.silu(normed * gamma + beta).astype(jnp.bfloat16)
    rimmed = extended_2(active, (("rows", 1),), 1)
    first_span = lax.axis_index("tm") == 0
    minus_one = jnp.where(first_span, rimmed, previous_span(rimmed))
    minus_two = jnp.where(first_span, rimmed, previous_span(minus_one))
    cache = jnp.concatenate([minus_two, minus_one], axis=0)
    extended = widen(jnp.concatenate([cache, rimmed], axis=0))
    columns = unfold(extended, height, across)
    conv = apply_taps(columns, lax.all_gather(kernel, "tm", axis=1, tiled=True), frames)
    return (values + conv + bias).astype(jnp.bfloat16)


def solution(mesh):
    in_specs = (P("tm", "rows", None, None), P(), P(), P(None, "tm", None, None, None), P())
    out_specs = P("tm", "rows", None, None)
    return jax.shard_map(local, mesh=mesh, in_specs=in_specs, out_specs=out_specs, check_vma=False)
```

profile of v0, /device:TPU:13, one launch (start us, length us, event | category | flops | bytes accessed | tf_op | source)
XLA Modules:
  0.0 135.2 jit_solution(9544178804054469499)
XLA Ops:
  6.5 0.0 copy-start
  6.5 0.0 copy-start.1
  6.5 0.0 copy-start.2
  6.5 0.0 all-gather.2.cloned.1.call-start
  6.5 6.1 %copy.9 = bf16[3,128,3,3,512]{1,4,3,2,0:T(8,128)(2,1)} copy(bf16[3,128,3,3,512]{4,1,3,2,0:T(8,128)(2,1)} %param.8) | data formatting | bytes 7077888 | tf_op args[3]
  12.6 0.0 all-gather.2.cloned.1.call-update
  12.6 0.0 copy-done
  12.6 0.1 convert_reduce_fusion
  12.7 0.1 reduce_sum.36
  12.8 0.1 reduce_sum.24
  12.9 0.1 reduce_sum.37
  13.0 0.1 reduce_sum.25
  13.1 40.4 %all-reduce.1 = (f32[32]{0:T(128)S(1)}, f32[32]{0:T(128)S(1)}) all-reduce(f32[32]{0:T(128)S(1)} %reduce_sum.37, f32[32]{0:T(128)S(1)} %reduce_sum.25), channel_id=1, replica_groups=mesh['tm'=4,'rows'=8] {'tm','rows'}, use_global_device_ids=true, to_apply=%region_5.6 | all-reduce | flops 64 | bytes 512 | tf_op jit(solution)/shard_map/psum | solution.py:76
  53.5 0.1 mul.43
  53.6 0.1 mul.44
  53.7 0.1 sub.19
  53.7 0.1 sub.20
  53.8 0.0 copy-done.1
  53.8 0.0 copy-done.2
  53.8 0.1 fusion.23
  54.0 3.0 %collective-permute-start.1 = (bf16[1,1,64,512]{3,2,1,0:T(8,128)(2,1)S(1)}, bf16[1,1,64,512]{3,2,1,0:T(8,128)(2,1)S(1)}, u32[]{:S(2)}, u32[]{:S(2)}) collective-permute-start(bf16[1,1,64,512]{3,2,1,0:T(8,128)(2,1)S(1)} %get-tuple-element.13), channel_id=1, source_target_pairs={{1,0},{2,1},{3,2},{4,3},{5,4},{6,5},{7,6},{9,8},{10,9},{11,10},{12... | collective-permute-start | bytes 196616 | tf_op jit(solution)/shard_map/ppermute | solution.py:24
  57.0 2.3 %collective-permute-start = (bf16[1,1,64,512]{3,2,1,0:T(8,128)(2,1)S(1)}, bf16[1,1,64,512]{3,2,1,0:T(8,128)(2,1)S(1)}, u32[]{:S(2)}, u32[]{:S(2)}) collective-permute-start(bf16[1,1,64,512]{3,2,1,0:T(8,128)(2,1)S(1)} %get-tuple-element.12), channel_id=1, source_target_pairs={{0,1},{1,2},{2,3},{3,4},{4,5},{5,6},{6,7},{8,9},{9,10},{10,11},{11... | collective-permute-start | bytes 196616 | tf_op jit(solution)/shard_map/ppermute | solution.py:23
  59.3 0.1 collective-permute-done.1
  59.4 3.5 %collective-permute-done = bf16[1,1,64,512]{3,2,1,0:T(8,128)(2,1)S(1)} collective-permute-done((bf16[1,1,64,512]{3,2,1,0:T(8,128)(2,1)S(1)}, bf16[1,1,64,512]{3,2,1,0:T(8,128)(2,1)S(1)}, u32[]{:S(2)}, u32[]{:S(2)}) %collective-permute-start) | collective-permute-done | bytes 65568 | tf_op jit(solution)/shard_map/ppermute | solution.py:23
  63.0 1.3 collective-permute-start.2
  64.3 5.3 %collective-permute-done.2 = bf16[1,5,64,512]{3,2,1,0:T(8,128)(2,1)S(1)} collective-permute-done((bf16[1,5,64,512]{3,2,1,0:T(8,128)(2,1)S(1)}, bf16[1,5,64,512]{3,2,1,0:T(8,128)(2,1)S(1)}, u32[]{:S(2)}, u32[]{:S(2)}) %collective-permute-start.2) | collective-permute-done | bytes 327712 | tf_op jit(solution)/shard_map/ppermute | solution.py:13
  69.7 1.3 collective-permute-start.3
  71.0 13.8 %collective-permute-done.3 = bf16[1,5,64,512]{3,2,1,0:T(8,128)(2,1)S(1)} collective-permute-done((bf16[1,5,64,512]{3,2,1,0:T(8,128)(2,1)S(1)}, bf16[1,5,64,512]{3,2,1,0:T(8,128)(2,1)S(1)}, u32[]{:S(2)}, u32[]{:S(2)}) %collective-permute-start.3) | collective-permute-done | bytes 327712 | tf_op jit(solution)/shard_map/ppermute | solution.py:13
  84.8 0.1 broadcast_select_fusion
  84.8 0.1 maximum_maximum_fusion
  84.9 1.0 fusion.9
  85.9 0.9 slice_dynamic-update-slice_fusion.2
  86.8 1.0 fusion.10
  87.8 1.0 fusion.11
  88.8 0.9 slice_dynamic-update-slice_fusion.1
  89.8 1.0 fusion.12
  90.8 1.0 fusion.13
  91.8 1.0 slice_dynamic-update-slice_fusion
  92.8 1.0 fusion.14
  93.8 20.4 %all-gather.2.cloned.1.call-done = bf16[3,512,3,3,512]{1,4,3,2,0:T(8,128)(2,1)} async-done(((bf16[3,128,3,3,512]{1,4,3,2,0:T(8,128)(2,1)}), bf16[3,512,3,3,512]{1,4,3,2,0:T(8,128)(2,1)}) %all-gather.2.cloned.1.call-update) | async-done | bytes 14155792 | tf_op jit(solution)/shard_map/all_gather | solution.py:94
  114.2 5.7 %fusion.25 = (bf16[1,512,3,3,512]{1,4,3,2,0:T(8,128)(2,1)S(1)}, bf16[1,512,3,3,512]{1,4,3,2,0:T(8,128)(2,1)S(1)}, bf16[1,512,3,3,512]{1,4,3,2,0:T(8,128)(2,1)S(1)}) fusion(bf16[3,512,3,3,512]{1,4,3,2,0:T(8,128)(2,1)} %all-gather.2.cloned.1.call-done), kind=kLoop, calls=%fused_computation.46 | loop fusion | bytes 28311552 | tf_op jit(solution)/shard_map/slice | solution.py:44
  120.0 2.5 %fusion = f32[3,64,512]{2,1,0:T(8,128)S(1)} fusion(bf16[512,4608,1]{0,1,2:T(8,128)(2,1)S(1)} %bitcast.43, bf16[3,3,64,4608]{3,2,1,0:T(8,128)(2,1)} %fusion.14), kind=kOutput, calls=%fused_computation.1 | convolution fusion | flops 905969664 | bytes 6881280 | tf_op jit(solution)/shard_map/fhwc,kc->fhwk/dot_general | solution.py:47
  122.5 0.0 copy-start.3
  122.5 2.6 %fusion.1 = f32[3,64,512]{2,1,0:T(8,128)S(1)} fusion(bf16[512,4608,1]{0,1,2:T(8,128)(2,1)S(1)} %bitcast.42, bf16[3,3,64,4608]{3,2,1,0:T(8,128)(2,1)} %fusion.14), kind=kOutput, calls=%fused_computation.3 | convolution fusion | flops 905969664 | bytes 6881280 | tf_op jit(solution)/shard_map/fhwc,kc->fhwk/dot_general | solution.py:47
  125.1 0.0 copy-done.3
  125.1 3.3 %fusion.8 = bf16[1,3,64,512]{3,2,1,0:T(8,128)(2,1)} fusion(f32[3,64,512]{2,1,0:T(8,128)S(1)} %fusion, f32[3,64,512]{2,1,0:T(8,128)S(1)} %fusion.1, bf16[512,4608,1]{0,1,2:T(8,128)(2,1)S(1)} %bitcast.41, bf16[3,3,64,4608]{3,2,1,0:T(8,128)(2,1)} %fusion.14, bf16[1,3,64,512]{3,2,1,0:T(8,128)(2,1)S(1)} %copy-done, f32[512]{0:T(512)S(1)} %copy-done.3), kind=kOutput, calls=%fused_computation.11 | convolution fusion | flops 906559488 | bytes 7669760 | tf_op jit(solution)/shard_map/fhwc,kc->fhwk/dot_general | solution.py:43
  (4 shorter events, 0.1 us)
Async XLA Ops:
  6.5 6.1 %copy-start = (bf16[1,3,64,512]{3,2,1,0:T(8,128)(2,1)S(1)}, bf16[1,3,64,512]{3,2,1,0:T(8,128)(2,1)}, u32[]{:S(2)}) copy-start(bf16[1,3,64,512]{3,2,1,0:T(8,128)(2,1)} %param.5) | copy-start | bytes 589828
  6.5 47.3 %copy-start.1 = (f32[512]{0:T(512)S(1)}, f32[512]{0:T(512)}, u32[]{:S(2)}) copy-start(f32[512]{0:T(512)} %param.7) | copy-start | bytes 6148
  6.5 47.3 %copy-start.2 = (f32[512]{0:T(512)S(1)}, f32[512]{0:T(512)}, u32[]{:S(2)}) copy-start(f32[512]{0:T(512)} %param.6) | copy-start | bytes 6148
  6.5 107.7 %all-gather.2.cloned.1.call-start = ((), (), s32[]{:S(2)}) async-start(), calls=%async_computation | async-start | bytes 17694720 | tf_op jit(solution)/shard_map/all_gather | solution.py:94
  54.0 5.4 %collective-permute-start.1 = (bf16[1,1,64,512]{3,2,1,0:T(8,128)(2,1)S(1)}, bf16[1,1,64,512]{3,2,1,0:T(8,128)(2,1)S(1)}, u32[]{:S(2)}, u32[]{:S(2)}) collective-permute-start(bf16[1,1,64,512]{3,2,1,0:T(8,128)(2,1)S(1)} %get-tuple-element.13), channel_id=1, source_target_pairs={{1,0},{2,1},{3,2},{4,3},{5,4},{6,5},{7,6},{9,8},{10,9},{11,10},{12... | collective-permute-start | bytes 196616 | tf_op jit(solution)/shard_map/ppermute | solution.py:24
  57.0 6.0 %collective-permute-start = (bf16[1,1,64,512]{3,2,1,0:T(8,128)(2,1)S(1)}, bf16[1,1,64,512]{3,2,1,0:T(8,128)(2,1)S(1)}, u32[]{:S(2)}, u32[]{:S(2)}) collective-permute-start(bf16[1,1,64,512]{3,2,1,0:T(8,128)(2,1)S(1)} %get-tuple-element.12), channel_id=1, source_target_pairs={{0,1},{1,2},{2,3},{3,4},{4,5},{5,6},{6,7},{8,9},{9,10},{10,11},{11... | collective-permute-start | bytes 196616 | tf_op jit(solution)/shard_map/ppermute | solution.py:23
  63.0 6.6 %collective-permute-start.2 = (bf16[1,5,64,512]{3,2,1,0:T(8,128)(2,1)S(1)}, bf16[1,5,64,512]{3,2,1,0:T(8,128)(2,1)S(1)}, u32[]{:S(2)}, u32[]{:S(2)}) collective-permute-start(bf16[1,5,64,512]{3,2,1,0:T(8,128)(2,1)S(1)} %pad_maximum_fusion), channel_id=1, source_target_pairs={{0,8},{8,16},{16,24},{1,9},{9,17},{17,25},{2,10},{10,18},{18,26},{... | collective-permute-start | bytes 983048 | tf_op jit(solution)/shard_map/ppermute | solution.py:13
  69.7 15.1 %collective-permute-start.3 = (bf16[1,5,64,512]{3,2,1,0:T(8,128)(2,1)S(1)}, bf16[1,5,64,512]{3,2,1,0:T(8,128)(2,1)S(1)}, u32[]{:S(2)}, u32[]{:S(2)}) collective-permute-start(bf16[1,5,64,512]{3,2,1,0:T(8,128)(2,1)S(1)} %broadcast_select_fusion.1), channel_id=1, source_target_pairs={{0,8},{8,16},{16,24},{1,9},{9,17},{17,25},{2,10},{10,18},{18,26},{... | collective-permute-start | bytes 983048 | tf_op jit(solution)/shard_map/ppermute | solution.py:13
  122.5 2.6 %copy-start.3 = (f32[512]{0:T(512)S(1)}, f32[512]{0:T(512)}, u32[]{:S(2)}) copy-start(f32[512]{0:T(512)} %param.9) | copy-start | bytes 6148
Sparse Core Ops, SparseCore 0:
  12.8 101.4 all-gather.1
where the time goes:
time: 136 us; the launch traced here: 135 us
  waiting for transfers between devices  43.1 us (32%)
  blocking collectives  40.4 us (30%)
  local copies, waits for them, and re-layouts  21.2 us (16%)
  between operations  13.5 us (10%)
  matrix products  8.36 us (6%)
  starting transfers between devices  7.87 us (6%)
    psum x1, blocking collectives, local(): lax.psum((jnp.sum(grouped, axis=(0, 1, 2, 4)), jnp.sum(grouped * grouped,...  40.4 us
    all_gather x1, waiting for transfers between devices, local(): lax.all_gather(kernel, 'tm', axis=1, tiled=True)  20.4 us
    ppermute x2, waiting for transfers between devices, shifted(): return lax.ppermute(x, axis, pairs)  19.1 us
    unnamed x17, local copies, waits for them, and re-layouts  14 us
    slice x1, local copies, waits for them, and re-layouts, apply_taps(): flat[0]  5.74 us
    dot_general x2, matrix products, apply_taps(): jnp.einsum('fhwc,kc->fhwk', columns[tap_time:tap_time + frames], flat[tap...  5.1 us
    ppermute x1, waiting for transfers between devices, extended_2(): before = lax.ppermute(last, axis, up)  3.54 us
    dot_general x1, matrix products, apply_taps(): jnp.einsum('fhwc,kc->fhwk', columns[0:frames], flat[0], preferred_element...  3.26 us
  transfers between devices with their start and end apart: 5, of which 5 were waited for; matrix products, arithmetic and copies ran while one was open for 7% of the time, Pallas kernels for 0%

commit v1 on v0

--- a/solution.py
+++ b/solution.py
@@ -91,7 +91,7 @@
     cache = jnp.concatenate([minus_two, minus_one], axis=0)
     extended = widen(jnp.concatenate([cache, rimmed], axis=0))
     columns = unfold(extended, height, across)
-    conv = apply_taps(columns, lax.all_gather(kernel, "tm", axis=1, tiled=True), frames)
+    conv = apply_taps(columns, jnp.concatenate(lax.all_gather(kernel, "tm"), axis=1), frames)
     return (values + conv + bias).astype(jnp.bfloat16)
 
 

time: 136 us -> 157 us (1.15)
  local copies, waits for them, and re-layouts: 21.2 us -> 41.5 us
  other arithmetic: 0.71 us -> 2.6 us
    all_gather x0 -> x1, local copies, waits for them, and re-layouts: none -> 22.4 us  [local(): lax.all_gather(kernel, 'tm')]
    unnamed x17 -> x12, local copies, waits for them, and re-layouts: 14 us -> 7.86 us
    slice x1, local copies, waits for them, and re-layouts: 5.74 us -> 9.72 us  [apply_taps(): flat[0]]
    all_gather x1, waiting for transfers between devices: 20.4 us -> 18.2 us  [local(): lax.all_gather(kernel, 'tm')]
  transfers between devices with their start and end apart: 5 -> 5, of which waited for: 5 -> 5; matrix products, arithmetic and copies ran while one was open for 7% -> 8% of each run, Pallas kernels for 0% -> 0%
where the time goes in v1:
time: 157 us; the launch traced here: 156 us
  waiting for transfers between devices  41.7 us (27%)
  local copies, waits for them, and re-layouts  41.5 us (26%)
  blocking collectives  40.4 us (26%)
  between operations  13.5 us (9%)
  matrix products  8.43 us (5%)
  starting transfers between devices  7.87 us (5%)
  other arithmetic  2.6 us (2%)
    psum x1, blocking collectives, local(): lax.psum((jnp.sum(grouped, axis=(0, 1, 2, 4)), jnp.sum(grouped * grouped,...  40.4 us
    all_gather x1, local copies, waits for them, and re-layouts, local(): lax.all_gather(kernel, 'tm')  22.4 us
    ppermute x2, waiting for transfers between devices, shifted(): return lax.ppermute(x, axis, pairs)  19.1 us
    all_gather x1, waiting for transfers between devices, local(): lax.all_gather(kernel, 'tm')  18.2 us
    slice x1, local copies, waits for them, and re-layouts, apply_taps(): flat[0]  9.72 us
    unnamed x12, local copies, waits for them, and re-layouts  7.86 us
    dot_general x2, matrix products, apply_taps(): jnp.einsum('fhwc,kc->fhwk', columns[tap_time:tap_time + frames], flat[tap...  5.15 us
    ppermute x1, waiting for transfers between devices, extended_2(): before = lax.ppermute(last, axis, up)  3.54 us
  transfers between devices with their start and end apart: 5, of which 5 were waited for; matrix products, arithmetic and copies ran while one was open for 8% of the time, Pallas kernels for 0%

profile of v1, /device:TPU:13, one launch (start us, length us, event | category | flops | bytes accessed | tf_op | source)
XLA Modules:
  0.0 156.0 jit_solution(17599423675937550427)
XLA Ops:
  6.5 0.0 all-gather.3.cloned.1.call-start
  6.5 0.7 all-gather.3.cloned.1.call-update
  7.3 1.0 convert_reduce_fusion
  8.3 0.1 reduce_sum.36
  8.3 0.1 reduce_sum.24
  8.4 0.1 reduce_sum.37
  8.5 0.1 reduce_sum.25
  8.7 40.4 %all-reduce.1 = (f32[32]{0:T(128)S(1)}, f32[32]{0:T(128)S(1)}) all-reduce(f32[32]{0:T(128)S(1)} %reduce_sum.37, f32[32]{0:T(128)S(1)} %reduce_sum.25), channel_id=1, replica_groups=mesh['tm'=4,'rows'=8] {'tm','rows'}, use_global_device_ids=true, to_apply=%region_5.6 | all-reduce | flops 64 | bytes 512 | tf_op jit(solution)/shard_map/psum | solution.py:76
  49.0 0.1 mul.43
  49.1 0.1 mul.44
  49.2 0.1 sub.19
  49.3 0.1 sub.20
  49.3 1.1 fusion.26
  50.5 3.0 %collective-permute-start.1 = (bf16[1,1,64,512]{3,2,1,0:T(8,128)(2,1)S(1)}, bf16[1,1,64,512]{3,2,1,0:T(8,128)(2,1)S(1)}, u32[]{:S(2)}, u32[]{:S(2)}) collective-permute-start(bf16[1,1,64,512]{3,2,1,0:T(8,128)(2,1)S(1)} %get-tuple-element.13), channel_id=1, source_target_pairs={{1,0},{2,1},{3,2},{4,3},{5,4},{6,5},{7,6},{9,8},{10,9},{11,10},{12... | collective-permute-start | bytes 196616 | tf_op jit(solution)/shard_map/ppermute | solution.py:24
  53.5 2.3 %collective-permute-start = (bf16[1,1,64,512]{3,2,1,0:T(8,128)(2,1)S(1)}, bf16[1,1,64,512]{3,2,1,0:T(8,128)(2,1)S(1)}, u32[]{:S(2)}, u32[]{:S(2)}) collective-permute-start(bf16[1,1,64,512]{3,2,1,0:T(8,128)(2,1)S(1)} %get-tuple-element.12), channel_id=1, source_target_pairs={{0,1},{1,2},{2,3},{3,4},{4,5},{5,6},{6,7},{8,9},{9,10},{10,11},{11... | collective-permute-start | bytes 196616 | tf_op jit(solution)/shard_map/ppermute | solution.py:23
  55.8 0.1 collective-permute-done.1
  55.9 3.5 %collective-permute-done = bf16[1,1,64,512]{3,2,1,0:T(8,128)(2,1)S(1)} collective-permute-done((bf16[1,1,64,512]{3,2,1,0:T(8,128)(2,1)S(1)}, bf16[1,1,64,512]{3,2,1,0:T(8,128)(2,1)S(1)}, u32[]{:S(2)}, u32[]{:S(2)}) %collective-permute-start) | collective-permute-done | bytes 65568 | tf_op jit(solution)/shard_map/ppermute | solution.py:23
  59.5 1.3 collective-permute-start.2
  60.8 4.9 %collective-permute-done.2 = bf16[1,5,64,512]{3,2,1,0:T(8,128)(2,1)S(1)} collective-permute-done((bf16[1,5,64,512]{3,2,1,0:T(8,128)(2,1)S(1)}, bf16[1,5,64,512]{3,2,1,0:T(8,128)(2,1)S(1)}, u32[]{:S(2)}, u32[]{:S(2)}) %collective-permute-start.2) | collective-permute-done | bytes 327712 | tf_op jit(solution)/shard_map/ppermute | solution.py:13
  65.7 1.3 collective-permute-start.3
  67.0 14.2 %collective-permute-done.3 = bf16[1,5,64,512]{3,2,1,0:T(8,128)(2,1)S(1)} collective-permute-done((bf16[1,5,64,512]{3,2,1,0:T(8,128)(2,1)S(1)}, bf16[1,5,64,512]{3,2,1,0:T(8,128)(2,1)S(1)}, u32[]{:S(2)}, u32[]{:S(2)}) %collective-permute-start.3) | collective-permute-done | bytes 327712 | tf_op jit(solution)/shard_map/ppermute | solution.py:13
  81.2 0.1 broadcast_select_fusion
  81.3 0.1 maximum_maximum_fusion
  81.4 1.0 fusion.12
  82.4 1.0 slice_dynamic-update-slice_fusion.2
  83.4 1.0 fusion.13
  84.4 1.0 fusion.14
  85.4 0.9 slice_dynamic-update-slice_fusion.1
  86.3 1.0 fusion.15
  87.3 1.0 fusion.16
  88.4 0.9 slice_dynamic-update-slice_fusion
  89.3 1.0 fusion.17
  90.3 18.2 %all-gather.3.cloned.1.call-done = bf16[12,128,3,3,512]{4,1,3,2,0:T(8,128)(2,1)} async-done(((bf16[3,128,3,3,512]{4,1,3,2,0:T(8,128)(2,1)}), bf16[12,128,3,3,512]{4,1,3,2,0:T(8,128)(2,1)}) %all-gather.3.cloned.1.call-update) | async-done | bytes 14155792 | tf_op jit(solution)/shard_map/all_gather | solution.py:94
  108.4 22.4 %copy.11 = bf16[4,3,128,3,3,512]{2,0,5,4,3,1:T(4,128)(2,1)} copy(bf16[4,3,128,3,3,512]{5,2,4,3,1,0:T(8,128)(2,1)} %bitcast.86) | data formatting | bytes 28311552 | tf_op jit(solution)/shard_map/all_gather | solution.py:94
  130.9 9.7 %fusion.28 = (bf16[1,4,128,3,3,512]{2,1,5,4,3,0:T(4,128)(2,1)S(1)}, bf16[1,4,128,3,3,512]{2,1,5,4,3,0:T(4,128)(2,1)S(1)}, bf16[1,4,128,3,3,512]{2,1,5,4,3,0:T(4,128)(2,1)S(1)}) fusion(bf16[3,4,128,3,3,512]{2,1,5,4,3,0:T(4,128)(2,1)} %bitcast.85), kind=kLoop, calls=%fused_computation.52 | loop fusion | bytes 28311552 | tf_op jit(solution)/shard_map/slice | solution.py:44
  140.6 2.6 %fusion = f32[3,64,512]{2,1,0:T(8,128)S(1)} fusion(bf16[576,8,4,128]{3,2,1,0:T(4,128)(2,1)S(1)} %bitcast.89, bf16[3,3,64,4608]{3,2,1,0:T(8,128)(2,1)} %fusion.17), kind=kOutput, calls=%fused_computation.1 | convolution fusion | flops 905969664 | bytes 6881280 | tf_op jit(solution)/shard_map/fhwc,kc->fhwk/dot_general | solution.py:47
  143.2 0.0 copy-start
  143.2 0.0 copy-start.1
  143.2 2.6 %fusion.2 = f32[3,64,512]{2,1,0:T(8,128)S(1)} fusion(bf16[576,8,4,128]{3,2,1,0:T(4,128)(2,1)S(1)} %bitcast.88, bf16[3,3,64,4608]{3,2,1,0:T(8,128)(2,1)} %fusion.17), kind=kOutput, calls=%fused_computation.4 | convolution fusion | flops 905969664 | bytes 6881280 | tf_op jit(solution)/shard_map/fhwc,kc->fhwk/dot_general | solution.py:47
  145.8 0.0 copy-done
  145.8 0.0 copy-done.1
  145.8 3.3 %fusion.11 = bf16[1,3,64,512]{3,2,1,0:T(8,128)(2,1)} fusion(f32[3,64,512]{2,1,0:T(8,128)S(1)} %fusion, f32[3,64,512]{2,1,0:T(8,128)S(1)} %fusion.2, bf16[576,8,4,128]{3,2,1,0:T(4,128)(2,1)S(1)} %bitcast.87, bf16[3,3,64,4608]{3,2,1,0:T(8,128)(2,1)} %fusion.17, bf16[1,3,64,512]{3,2,1,0:T(8,128)(2,1)S(1)} %copy-done, f32[512]{0:T(512)S(1)} %copy-done.1), kind=kOutput, calls=%fused_computation.17 | convolution fusion | flops 906559488 | bytes 7669760 | tf_op jit(solution)/shard_map/fhwc,kc->fhwk/dot_general | solution.py:43
  (4 shorter events, 0.1 us)
Async XLA Ops:
  6.5 101.9 %all-gather.3.cloned.1.call-start = ((), (), s32[]{:S(2)}) async-start(), calls=%async_computation | async-start | bytes 17694720 | tf_op jit(solution)/shard_map/all_gather | solution.py:94
  50.5 5.4 %collective-permute-start.1 = (bf16[1,1,64,512]{3,2,1,0:T(8,128)(2,1)S(1)}, bf16[1,1,64,512]{3,2,1,0:T(8,128)(2,1)S(1)}, u32[]{:S(2)}, u32[]{:S(2)}) collective-permute-start(bf16[1,1,64,512]{3,2,1,0:T(8,128)(2,1)S(1)} %get-tuple-element.13), channel_id=1, source_target_pairs={{1,0},{2,1},{3,2},{4,3},{5,4},{6,5},{7,6},{9,8},{10,9},{11,10},{12... | collective-permute-start | bytes 196616 | tf_op jit(solution)/shard_map/ppermute | solution.py:24
  53.5 6.0 %collective-permute-start = (bf16[1,1,64,512]{3,2,1,0:T(8,128)(2,1)S(1)}, bf16[1,1,64,512]{3,2,1,0:T(8,128)(2,1)S(1)}, u32[]{:S(2)}, u32[]{:S(2)}) collective-permute-start(bf16[1,1,64,512]{3,2,1,0:T(8,128)(2,1)S(1)} %get-tuple-element.12), channel_id=1, source_target_pairs={{0,1},{1,2},{2,3},{3,4},{4,5},{5,6},{6,7},{8,9},{9,10},{10,11},{11... | collective-permute-start | bytes 196616 | tf_op jit(solution)/shard_map/ppermute | solution.py:23
  59.5 6.2 %collective-permute-start.2 = (bf16[1,5,64,512]{3,2,1,0:T(8,128)(2,1)S(1)}, bf16[1,5,64,512]{3,2,1,0:T(8,128)(2,1)S(1)}, u32[]{:S(2)}, u32[]{:S(2)}) collective-permute-start(bf16[1,5,64,512]{3,2,1,0:T(8,128)(2,1)S(1)} %pad_maximum_fusion), channel_id=1, source_target_pairs={{0,8},{8,16},{16,24},{1,9},{9,17},{17,25},{2,10},{10,18},{18,26},{... | collective-permute-start | bytes 983048 | tf_op jit(solution)/shard_map/ppermute | solution.py:13
  65.7 15.5 %collective-permute-start.3 = (bf16[1,5,64,512]{3,2,1,0:T(8,128)(2,1)S(1)}, bf16[1,5,64,512]{3,2,1,0:T(8,128)(2,1)S(1)}, u32[]{:S(2)}, u32[]{:S(2)}) collective-permute-start(bf16[1,5,64,512]{3,2,1,0:T(8,128)(2,1)S(1)} %broadcast_select_fusion.1), channel_id=1, source_target_pairs={{0,8},{8,16},{16,24},{1,9},{9,17},{17,25},{2,10},{10,18},{18,26},{... | collective-permute-start | bytes 983048 | tf_op jit(solution)/shard_map/ppermute | solution.py:13
  143.2 2.6 %copy-start = (bf16[1,3,64,512]{3,2,1,0:T(8,128)(2,1)S(1)}, bf16[1,3,64,512]{3,2,1,0:T(8,128)(2,1)}, u32[]{:S(2)}) copy-start(bf16[1,3,64,512]{3,2,1,0:T(8,128)(2,1)} %param.5) | copy-start | bytes 589828
  143.2 2.6 %copy-start.1 = (f32[512]{0:T(512)S(1)}, f32[512]{0:T(512)}, u32[]{:S(2)}) copy-start(f32[512]{0:T(512)} %param.9) | copy-start | bytes 6148
Sparse Core Ops, SparseCore 0:
  8.9 99.5 all-gather.2
